TPU v7x, 32 devices: a whole 2x2x4 slice. The times are simulated.
32 devices in a mesh: pool: 4 (over y, core), ga: 8 (over z, x).
Axes of the slice: x: 2, y: 2, z: 4, core: 2. Of those that a mesh axis runs over, the one named last changes fastest.
Arguments:
- coefficients: bfloat16 [4, 256, 2, 256, 128], P('pool', 'ga'), may hold values from -6 to 6
- stick_count: int32 [4, 8], P('pool', 'ga'), may hold values from 28 to 32, as said below
- dest_device: int32 [4, 256], P('pool', 'ga'), may hold values from -1 to 7, as said below
- dest_slot: int32 [4, 256], P('pool', 'ga'), may hold values from -1 to 31, as said below
- source_stick: int32 [4, 256], P('pool', 'ga'), may hold values from -1 to 255, as said below
Outputs:
- margins: float32 [4, 2, 256, 256], P('pool', None, 'ga')
Inputs may be any that keep to these rules, and one draw needn't show every extreme that they name: Every k-point has a device whose 32 slots are all live; a device's live sticks are its first stick_count slots. `dest_device`: -1 exactly for sticks that land nowhere (among them all sticks that are not live); no device sends more than 8 of its sticks to one device, and some pair of devices reaches 8 for every k-point. `dest_slot`: -1 where dest_device is -1; the slots named are live slots of the layout of k-point q-1, no slot named twice. `source_stick`: the exact inverse of dest_device and dest_slot: a slot names a stick exactly when that stick names the slot, else -1.
All inputs are finite; a program needn't handle non-finite values.
Results may differ from a plain program's by a relative error of at most 0.0003.
Values may be sent and summed in bfloat16 or wider, within the bound.
No kernel may reach another device: no remote copies, remote signals or barrier semaphores. Data moves between devices by JAX's collectives and lax.ppermute only.
A program may use at most 64 MiB of HBM per device.

v0:
```python
import jax
import jax.numpy as jnp
from jax import lax
from jax.sharding import PartitionSpec as P


def passed_along(value, axis, steps):
    count = lax.axis_size(axis)
    pairs = [(source, (source + steps) % count) for source in range(count)]
    return lax.ppermute(value, axis, pairs)


def margin(bra_rows, ket_rows, slot_count, bands, plane_waves):
    bra_block = bra_rows.reshape(slot_count, 2, bands, plane_waves)
    ket_block = ket_rows.reshape(slot_count, 2, bands, plane_waves)
    swapped = jnp.stack([ket_block[:, 1], -ket_block[:, 0]], axis=1)
    real_part = jnp.einsum(
        "scmg,scng->mn", bra_block, ket_block, preferred_element_type=jnp.float32
    )
    imag_part = jnp.einsum("scmg,scng->mn", bra_block, swapped, preferred_element_type=jnp.float32)
    return jnp.stack([real_part, imag_part])


def owner_rows(partial_value, groups, bands, norm_scale):
    row_count = bands // groups
    totals = lax.psum(partial_value, "ga")
    owned = lax.dynamic_slice_in_dim(totals, lax.axis_index("ga") * row_count, row_count, 1)
    return owned * norm_scale


def local(coefficients, stick_count, dest_device, dest_slot, source_stick):
    groups = lax.axis_size("ga")
    slot_count = coefficients.shape[1]
    bands = coefficients.shape[3]
    plane_waves = coefficients.shape[4]
    pair_cap = max(2, (2 * slot_count + groups - 1) // groups)
    buffer_rows = groups * pair_cap
    norm_scale = (2 * groups * slot_count * plane_waves) ** (-0.5)
    coef_rows = coefficients.reshape(slot_count, -1)
    slot_list = jnp.arange(slot_count, dtype=jnp.int32)
    buffer_list = jnp.arange(buffer_rows, dtype=jnp.int32)
    live_mask = slot_list < stick_count[0, 0]
    bra_rows = jnp.where(live_mask[:, None], coef_rows, jnp.zeros_like(coef_rows))
    targets = dest_device[0]
    dest_order = dest_slot[0]
    matching = targets[:, None] == targets[None, :]
    earlier = dest_order[None, :] < dest_order[:, None]
    ranking = jnp.sum((matching & earlier).astype(jnp.int32), axis=1)
    position = jnp.where(targets >= 0, targets * pair_cap + ranking, -1)
    packer = (buffer_list[:, None] == position[None, :]).astype(jnp.bfloat16)
    outgoing = jnp.dot(packer, coef_rows, preferred_element_type=jnp.float32).astype(jnp.bfloat16)
    outgoing = outgoing.reshape(groups, pair_cap, -1)
    incoming = lax.all_to_all(outgoing, "ga", split_axis=0, concat_axis=0, tiled=True)
    anchor = source_stick[0]
    source_dev = jnp.where(anchor >= 0, anchor // slot_count, -1)
    matching_in = source_dev[:, None] == source_dev[None, :]
    earlier_in = slot_list[None, :] < slot_list[:, None]
    ranking_in = jnp.sum((matching_in & earlier_in).astype(jnp.int32), axis=1)
    position_in = jnp.where(anchor >= 0, source_dev * pair_cap + ranking_in, -1)
    placer = (position_in[:, None] == buffer_list[None, :]).astype(jnp.bfloat16)
    ket_rows = jnp.dot(
        placer, incoming.reshape(buffer_rows, -1), preferred_element_type=jnp.float32
    ).astype(jnp.bfloat16)
    bra_here = passed_along(bra_rows, "pool", 1)
    partial_value = margin(bra_here, ket_rows, slot_count, bands, plane_waves)
    finished = owner_rows(partial_value, groups, bands, norm_scale)
    result = passed_along(finished, "pool", -1)
    return result[None]


def solution(mesh):
    return jax.shard_map(
        local,
        mesh=mesh,
        in_specs=(
            P("pool", "ga", None, None, None),
            P("pool", "ga"),
            P("pool", "ga"),
            P("pool", "ga"),
            P("pool", "ga"),
        ),
        out_specs=P("pool", None, "ga", None),
        check_vma=False,
    )
```

profile of v0, /device:TPU:1, one launch (start us, length us, event | category | flops | bytes accessed | tf_op | source)
XLA Modules:
  0.0 305.1 jit_solution(17752583700953156419)
XLA Ops:
  6.5 5.6 %reshape.71 = bf16[32,65536]{1,0:T(8,128)(2,1)} reshape(bf16[1,32,2,256,128]{4,3,2,1,0:T(8,128)(2,1)} %param.5) | data formatting | bytes 8388608 | tf_op jit(solution)/shard_map/reshape | solution.py:39
  12.1 0.2 convert_reduce_fusion
  12.3 7.7 %fusion = bf16[8,8,65536]{2,1,0:T(8,128)(2,1)} fusion(bf16[32,65536]{1,0:T(8,128)(2,1)} %reshape.71, s32[32]{0:T(128)S(1)} %fusion.23), kind=kOutput, calls=%fused_computation.1 | convolution fusion | flops 272631808 | bytes 12583040 | tf_op jit(solution)/shard_map/dot_general | solution.py:51
  20.0 6.3 %all-to-all-start = ((bf16[8,8,65536]{2,1,0:T(8,128)(2,1)}), bf16[8,8,65536]{2,1,0:T(8,128)(2,1)}, u32[]{:S(2)}, u32[]{:S(2)}) async-start(bf16[8,8,65536]{2,1,0:T(8,128)(2,1)} %fusion), calls=%async_computation | async-start | bytes 16777216 | tf_op jit(solution)/shard_map/all_to_all | solution.py:53
  26.4 0.0 all-reduce.2.cloned.1.call-start
  27.1 2.5 broadcast_select_fusion
  29.6 2.1 collective-permute-start
  31.8 0.2 convert_reduce_fusion.1
  32.0 45.2 %collective-permute-done = bf16[32,65536]{1,0:T(8,128)(2,1)S(1)} collective-permute-done((bf16[32,65536]{1,0:T(8,128)(2,1)S(1)}, bf16[32,65536]{1,0:T(8,128)(2,1)S(1)}, u32[]{:S(2)}, u32[]{:S(2)}) %collective-permute-start) | collective-permute-done | bytes 4194336 | tf_op jit(solution)/shard_map/ppermute | solution.py:10
  77.2 2.9 copy.21
  80.1 128.7 %all-to-all-done = bf16[8,8,65536]{2,1,0:T(8,128)(2,1)} async-done(((bf16[8,8,65536]{2,1,0:T(8,128)(2,1)}), bf16[8,8,65536]{2,1,0:T(8,128)(2,1)}, u32[]{:S(2)}, u32[]{:S(2)}) %all-to-all-start) | async-done | bytes 8388640 | tf_op jit(solution)/shard_map/all_to_all | solution.py:53
  208.7 4.7 %fusion.9 = bf16[4,8,512,128]{3,1,2,0:T(8,128)(2,1)S(1)} fusion(bf16[8,8,65536]{2,1,0:T(8,128)(2,1)} %all-to-all-done, s32[32]{0:T(128)S(1)} %compare_select_fusion.8), kind=kOutput, calls=%fused_computation.12 | convolution fusion | flops 270534656 | bytes 12583040 | tf_op jit(solution)/shard_map/dot_general | solution.py:61
  213.4 1.0 copy.22
  214.4 0.8 fusion.27
  215.2 1.4 copy-done
  216.6 1.3 fusion.12
  217.9 1.3 fusion.15
  219.1 0.8 pad_maximum_fusion
  220.0 0.0 all-reduce.2.cloned.1.call-update
  220.0 71.4 %all-reduce.2.cloned.1.call-done = f32[2,256,256]{2,1,0:T(8,128)} async-done(((f32[2,256,256]{2,1,0:T(8,128)}), f32[2,256,256]{2,1,0:T(8,128)}) %all-reduce.2.cloned.1.call-update) | async-done | bytes 524304 | tf_op jit(solution)/shard_map/psum | solution.py:26
  291.4 0.8 dynamic-slice_multiply_fusion
  292.2 2.4 collective-permute-start.1
  294.6 3.0 collective-permute-done.1
  297.6 0.6 copy.38
  (12 shorter events, 0.1 us)
Async XLA Ops:
  6.5 5.6 %copy-start.2 = (s32[1,32]{1,0:T(1,128)S(1)}, s32[1,32]{1,0:T(1,128)}, u32[]{:S(2)}) copy-start(s32[1,32]{1,0:T(1,128)} %param.7) | copy-start | bytes 388
  6.5 5.6 %copy-start.1 = (s32[1,32]{1,0:T(1,128)S(1)}, s32[1,32]{1,0:T(1,128)}, u32[]{:S(2)}) copy-start(s32[1,32]{1,0:T(1,128)} %param.8) | copy-start | bytes 388
  20.0 188.7 %all-to-all-start = ((bf16[8,8,65536]{2,1,0:T(8,128)(2,1)}), bf16[8,8,65536]{2,1,0:T(8,128)(2,1)}, u32[]{:S(2)}, u32[]{:S(2)}) async-start(bf16[8,8,65536]{2,1,0:T(8,128)(2,1)} %fusion), calls=%async_computation | async-start | bytes 16777216 | tf_op jit(solution)/shard_map/all_to_all | solution.py:53
  26.4 265.0 %all-reduce.2.cloned.1.call-start = ((), (), s32[]{:S(2)}) async-start(), calls=%async_computation.1 | async-start | bytes 1048576 | tf_op jit(solution)/shard_map/psum | solution.py:26
  27.1 4.7 %copy-start.3 = (s32[1,32]{1,0:T(1,128)S(1)}, s32[1,32]{1,0:T(1,128)}, u32[]{:S(2)}) copy-start(s32[1,32]{1,0:T(1,128)} %param.9) | copy-start | bytes 388
  29.6 47.6 %collective-permute-start = (bf16[32,65536]{1,0:T(8,128)(2,1)S(1)}, bf16[32,65536]{1,0:T(8,128)(2,1)S(1)}, u32[]{:S(2)}, u32[]{:S(2)}) collective-permute-start(bf16[32,65536]{1,0:T(8,128)(2,1)S(1)} %broadcast_select_fusion), channel_id=1, source_target_pairs={{0,8},{8,16},{16,24},{24,0},{1,9},{9,17},{17,25},{25,1},{2,10},{10... | collective-permute-start | bytes 12582920 | tf_op jit(solution)/shard_map/ppermute | solution.py:10
  214.4 2.2 copy-start
  292.2 5.4 %collective-permute-start.1 = (f32[2,32,256]{2,1,0:T(8,128)S(1)}, f32[2,32,256]{2,1,0:T(8,128)S(1)}, u32[]{:S(2)}, u32[]{:S(2)}) collective-permute-start(f32[2,32,256]{2,1,0:T(8,128)S(1)} %dynamic-slice_multiply_fusion), channel_id=1, source_target_pairs={{0,24},{8,0},{16,8},{24,16},{1,25},{9,1},{17,9},{25,17},{2,26},{10... | collective-permute-start | bytes 196616 | tf_op jit(solution)/shard_map/ppermute | solution.py:10
Sparse Core Ops, SparseCore 0:
  220.1 71.2 all-reduce.1
where the time goes:
time: 306 us; the launch traced here: 305 us
  waiting for transfers between devices  248 us (81%)
  matrix products  15 us (5%)
  between operations  14.1 us (5%)
  local copies, waits for them, and re-layouts  11.5 us (4%)
  starting transfers between devices  10.9 us (4%)
  other arithmetic  5.37 us (2%)
    all_to_all x1, waiting for transfers between devices, local(): lax.all_to_all(outgoing, 'ga', split_axis=0, concat_axis=0, tiled=True)  129 us
    psum x1, waiting for transfers between devices, owner_rows(): totals = lax.psum(partial_value, 'ga')  71.4 us
    ppermute x2, waiting for transfers between devices, passed_along(): return lax.ppermute(value, axis, pairs)  48.2 us
    dot_general x1, matrix products, local(): jnp.dot(packer, coef_rows, preferred_element_type=jnp.float32)  7.73 us
    all_to_all x1, starting transfers between devices, local(): lax.all_to_all(outgoing, 'ga', split_axis=0, concat_axis=0, tiled=True)  6.34 us
  transfers between devices with their start and end apart: 4, of which 4 were waited for; matrix products, arithmetic and copies ran while one was open for 2% of the time, Pallas kernels for 0%

commit v1 on v0

--- a/solution.py
+++ b/solution.py
@@ -23,7 +23,9 @@
 
 def owner_rows(partial_value, groups, bands, norm_scale):
     row_count = bands // groups
-    totals = lax.psum(partial_value, "ga")
+    totals = partial_value
+    for hop in (1, 2, 4):
+        totals = totals + lax.ppermute(totals, "ga", [(dev, dev ^ hop) for dev in range(8)])
     owned = lax.dynamic_slice_in_dim(totals, lax.axis_index("ga") * row_count, row_count, 1)
     return owned * norm_scale
 

time: 306 us -> 269 us (0.88)
  waiting for transfers between devices: 248 us -> 220 us
  between operations: 14.1 us -> 0.76 us
  starting transfers between devices: 10.9 us -> 17.3 us
    psum x1 -> x0, waiting for transfers between devices: 71.4 us -> none  [owner_rows(): totals = lax.psum(partial_value, 'ga')]
    ppermute x0 -> x3, waiting for transfers between devices: none -> 43 us  [owner_rows(): lax.ppermute(totals, 'ga', [(dev, dev ^ hop) for dev in range(8)])]
    ppermute x0 -> x3, starting transfers between devices: none -> 7.41 us  [owner_rows(): lax.ppermute(totals, 'ga', [(dev, dev ^ hop) for dev in range(8)])]
  transfers between devices with their start and end apart: 4 -> 6, of which waited for: 4 -> 6; matrix products, arithmetic and copies ran while one was open for 2% -> 2% of each run, Pallas kernels for 0% -> 0%
where the time goes in v1:
time: 269 us; the launch traced here: 268 us
  waiting for transfers between devices  220 us (82%)
  starting transfers between devices  17.3 us (6%)
  matrix products  15 us (6%)
  local copies, waits for them, and re-layouts  11.4 us (4%)
  other arithmetic  3.95 us (1%)
    all_to_all x1, waiting for transfers between devices, local(): lax.all_to_all(outgoing, 'ga', split_axis=0, concat_axis=0, tiled=True)  129 us
    ppermute x2, waiting for transfers between devices, passed_along(): return lax.ppermute(value, axis, pairs)  48.3 us
    ppermute x3, waiting for transfers between devices, owner_rows(): lax.ppermute(totals, 'ga', [(dev, dev ^ hop) for dev in range(8)])  43 us
    dot_general x1, matrix products, local(): jnp.dot(packer, coef_rows, preferred_element_type=jnp.float32)  7.72 us
    ppermute x3, starting transfers between devices, owner_rows(): lax.ppermute(totals, 'ga', [(dev, dev ^ hop) for dev in range(8)])  7.41 us
    all_to_all x1, starting transfers between devices, local(): lax.all_to_all(outgoing, 'ga', split_axis=0, concat_axis=0, tiled=True)  6.34 us
    unnamed x11, local copies, waits for them, and re-layouts  5.86 us
    reshape x1, local copies, waits for them, and re-layouts, local(): coef_rows = coefficients.reshape(slot_count, -1)  5.57 us
  transfers between devices with their start and end apart: 6, of which 6 were waited for; matrix products, arithmetic and copies ran while one was open for 2% of the time, Pallas kernels for 0%

profile of v1, /device:TPU:1, one launch (start us, length us, event | category | flops | bytes accessed | tf_op | source)
XLA Modules:
  0.0 268.4 jit_solution(7769267728742006105)
XLA Ops:
  0.0 5.6 %reshape.71 = bf16[32,65536]{1,0:T(8,128)(2,1)} reshape(bf16[1,32,2,256,128]{4,3,2,1,0:T(8,128)(2,1)} %param.5) | data formatting | bytes 8388608 | tf_op jit(solution)/shard_map/reshape | solution.py:41
  5.8 7.7 %fusion = bf16[8,8,65536]{2,1,0:T(8,128)(2,1)} fusion(bf16[32,65536]{1,0:T(8,128)(2,1)} %reshape.71, s32[32]{0:T(128)S(1)} %get-tuple-element.7), kind=kOutput, calls=%fused_computation.1 | convolution fusion | flops 272631808 | bytes 12583040 | tf_op jit(solution)/shard_map/dot_general | solution.py:53
  13.5 6.3 %all-to-all-start = ((bf16[8,8,65536]{2,1,0:T(8,128)(2,1)}), bf16[8,8,65536]{2,1,0:T(8,128)(2,1)}, u32[]{:S(2)}, u32[]{:S(2)}) async-start(bf16[8,8,65536]{2,1,0:T(8,128)(2,1)} %fusion), calls=%async_computation | async-start | bytes 16777216 | tf_op jit(solution)/shard_map/all_to_all | solution.py:55
  20.5 2.5 broadcast_select_fusion
  23.1 2.1 collective-permute-start
  25.2 0.2 convert_reduce_fusion.1
  25.4 45.2 %collective-permute-done = bf16[32,65536]{1,0:T(8,128)(2,1)S(1)} collective-permute-done((bf16[32,65536]{1,0:T(8,128)(2,1)S(1)}, bf16[32,65536]{1,0:T(8,128)(2,1)S(1)}, u32[]{:S(2)}, u32[]{:S(2)}) %collective-permute-start) | collective-permute-done | bytes 4194336 | tf_op jit(solution)/shard_map/ppermute | solution.py:10
  70.6 2.9 %copy.21 = bf16[4,8,512,128]{3,2,1,0:T(8,128)(2,1)} copy(bf16[4,8,512,128]{3,1,2,0:T(8,128)(2,1)S(1)} %bitcast.57) | data formatting | bytes 8388608
  73.5 128.7 %all-to-all-done = bf16[8,8,65536]{2,1,0:T(8,128)(2,1)} async-done(((bf16[8,8,65536]{2,1,0:T(8,128)(2,1)}), bf16[8,8,65536]{2,1,0:T(8,128)(2,1)}, u32[]{:S(2)}, u32[]{:S(2)}) %all-to-all-start) | async-done | bytes 8388640 | tf_op jit(solution)/shard_map/all_to_all | solution.py:55
  202.2 4.7 %fusion.9 = bf16[4,8,512,128]{3,1,2,0:T(8,128)(2,1)S(1)} fusion(bf16[8,8,65536]{2,1,0:T(8,128)(2,1)} %all-to-all-done, s32[32]{0:T(128)S(1)} %compare_select_fusion.8), kind=kOutput, calls=%fused_computation.12 | convolution fusion | flops 270534656 | bytes 12583040 | tf_op jit(solution)/shard_map/dot_general | solution.py:63
  206.9 1.0 copy.22
  207.9 0.8 fusion.29
  208.7 1.4 copy-done
  210.1 1.3 fusion.12
  211.4 1.3 fusion.15
  212.7 1.6 collective-permute-start.1
  214.3 10.3 %collective-permute-done.1 = f32[2,256,256]{2,1,0:T(8,128)S(1)} collective-permute-done((f32[2,256,256]{2,1,0:T(8,128)S(1)}, f32[2,256,256]{2,1,0:T(8,128)S(1)}, u32[]{:S(2)}, u32[]{:S(2)}) %collective-permute-start.1) | collective-permute-done | bytes 524320 | tf_op jit(solution)/shard_map/ppermute | solution.py:28
  224.7 1.6 collective-permute-start.2
  226.3 9.9 %collective-permute-done.2 = f32[2,256,256]{2,1,0:T(8,128)S(1)} collective-permute-done((f32[2,256,256]{2,1,0:T(8,128)S(1)}, f32[2,256,256]{2,1,0:T(8,128)S(1)}, u32[]{:S(2)}, u32[]{:S(2)}) %collective-permute-start.2) | collective-permute-done | bytes 524320 | tf_op jit(solution)/shard_map/ppermute | solution.py:28
  236.4 4.2 %collective-permute-start.3 = (f32[2,256,256]{2,1,0:T(8,128)S(1)}, f32[2,256,256]{2,1,0:T(8,128)S(1)}, u32[]{:S(2)}, u32[]{:S(2)}) collective-permute-start(f32[2,256,256]{2,1,0:T(8,128)S(1)} %fusion.31), channel_id=1, source_target_pairs={{0,4},{1,5},{2,6},{3,7},{4,0},{5,1},{6,2},{7,3},{8,12},{9,13},{10,... | collective-permute-start | bytes 1572872 | tf_op jit(solution)/shard_map/ppermute | solution.py:28
  240.6 22.7 %collective-permute-done.3 = f32[2,256,256]{2,1,0:T(8,128)S(1)} collective-permute-done((f32[2,256,256]{2,1,0:T(8,128)S(1)}, f32[2,256,256]{2,1,0:T(8,128)S(1)}, u32[]{:S(2)}, u32[]{:S(2)}) %collective-permute-start.3) | collective-permute-done | bytes 524320 | tf_op jit(solution)/shard_map/ppermute | solution.py:28
  263.3 1.4 collective-permute-start.4
  264.8 3.0 %collective-permute-done.4 = f32[2,32,256]{2,1,0:T(8,128)S(1)} collective-permute-done((f32[2,32,256]{2,1,0:T(8,128)S(1)}, f32[2,32,256]{2,1,0:T(8,128)S(1)}, u32[]{:S(2)}, u32[]{:S(2)}) %collective-permute-start.4) | collective-permute-done | bytes 65568 | tf_op jit(solution)/shard_map/ppermute | solution.py:10
  267.8 0.6 copy.37
  (16 shorter events, 0.5 us)
Async XLA Ops:
  0.0 5.6 %copy-start.1 = (s32[1,32]{1,0:T(1,128)S(1)}, s32[1,32]{1,0:T(1,128)}, u32[]{:S(2)}) copy-start(s32[1,32]{1,0:T(1,128)} %param.7) | copy-start | bytes 388
  0.0 5.6 %copy-start.2 = (s32[1,32]{1,0:T(1,128)S(1)}, s32[1,32]{1,0:T(1,128)}, u32[]{:S(2)}) copy-start(s32[1,32]{1,0:T(1,128)} %param.8) | copy-start | bytes 388
  0.0 5.8 %copy-start.3 = (s32[1,32]{1,0:T(1,128)S(1)}, s32[1,32]{1,0:T(1,128)}, u32[]{:S(2)}) copy-start(s32[1,32]{1,0:T(1,128)} %param.9) | copy-start | bytes 388
  13.5 188.7 %all-to-all-start = ((bf16[8,8,65536]{2,1,0:T(8,128)(2,1)}), bf16[8,8,65536]{2,1,0:T(8,128)(2,1)}, u32[]{:S(2)}, u32[]{:S(2)}) async-start(bf16[8,8,65536]{2,1,0:T(8,128)(2,1)} %fusion), calls=%async_computation | async-start | bytes 16777216 | tf_op jit(solution)/shard_map/all_to_all | solution.py:55
  23.1 47.6 %collective-permute-start = (bf16[32,65536]{1,0:T(8,128)(2,1)S(1)}, bf16[32,65536]{1,0:T(8,128)(2,1)S(1)}, u32[]{:S(2)}, u32[]{:S(2)}) collective-permute-start(bf16[32,65536]{1,0:T(8,128)(2,1)S(1)} %broadcast_select_fusion), channel_id=1, source_target_pairs={{0,8},{8,16},{16,24},{24,0},{1,9},{9,17},{17,25},{25,1},{2,10},{10... | collective-permute-start | bytes 12582920 | tf_op jit(solution)/shard_map/ppermute | solution.py:10
  207.9 2.2 copy-start
  212.7 12.0 %collective-permute-start.1 = (f32[2,256,256]{2,1,0:T(8,128)S(1)}, f32[2,256,256]{2,1,0:T(8,128)S(1)}, u32[]{:S(2)}, u32[]{:S(2)}) collective-permute-start(f32[2,256,256]{2,1,0:T(8,128)S(1)} %pad_maximum_fusion), channel_id=1, source_target_pairs={{0,1},{1,0},{2,3},{3,2},{4,5},{5,4},{6,7},{7,6},{8,9},{9,8},{10,11... | collective-permute-start | bytes 1572872 | tf_op jit(solution)/shard_map/ppermute | solution.py:28
  224.7 11.6 %collective-permute-start.2 = (f32[2,256,256]{2,1,0:T(8,128)S(1)}, f32[2,256,256]{2,1,0:T(8,128)S(1)}, u32[]{:S(2)}, u32[]{:S(2)}) collective-permute-start(f32[2,256,256]{2,1,0:T(8,128)S(1)} %fusion.27), channel_id=1, source_target_pairs={{0,2},{1,3},{2,0},{3,1},{4,6},{5,7},{6,4},{7,5},{8,10},{9,11},{10,... | collective-permute-start | bytes 1572872 | tf_op jit(solution)/shard_map/ppermute | solution.py:28
  236.4 26.9 %collective-permute-start.3 = (f32[2,256,256]{2,1,0:T(8,128)S(1)}, f32[2,256,256]{2,1,0:T(8,128)S(1)}, u32[]{:S(2)}, u32[]{:S(2)}) collective-permute-start(f32[2,256,256]{2,1,0:T(8,128)S(1)} %fusion.31), channel_id=1, source_target_pairs={{0,4},{1,5},{2,6},{3,7},{4,0},{5,1},{6,2},{7,3},{8,12},{9,13},{10,... | collective-permute-start | bytes 1572872 | tf_op jit(solution)/shard_map/ppermute | solution.py:28
  263.3 4.5 %collective-permute-start.4 = (f32[2,32,256]{2,1,0:T(8,128)S(1)}, f32[2,32,256]{2,1,0:T(8,128)S(1)}, u32[]{:S(2)}, u32[]{:S(2)}) collective-permute-start(f32[2,32,256]{2,1,0:T(8,128)S(1)} %fusion.20), channel_id=1, source_target_pairs={{0,24},{8,0},{16,8},{24,16},{1,25},{9,1},{17,9},{25,17},{2,26},{10... | collective-permute-start | bytes 196616 | tf_op jit(solution)/shard_map/ppermute | solution.py:10
